TPU v7x, 256 devices: a whole 4x4x8 slice. The times are simulated.
256 devices in a mesh: row: 16 (over y, x), col: 8 (over z), rep: 2 (over core).
Axes of the slice: x: 4, y: 4, z: 8, core: 2. Of those that a mesh axis runs over, the one named last changes fastest.
Arguments:
- patches: bfloat16 [2, 512, 6144], P('rep', 'col', 'row'), may hold values from -6 to 6
- cotangent: bfloat16 [2, 512, 6144], P('rep', 'col', 'row'), may hold values from -6 to 6
- w_in: bfloat16 [6144, 24576], P('row', 'col'), may hold values from -0.078125 to 0.078125
- w_out: bfloat16 [24576, 6144], P('col', 'row'), may hold values from -0.0390625 to 0.0390625
- moment_in: bfloat16 [2, 6144, 24576], P('rep', 'row', 'col'), may hold values from -2 to 2
- moment_out: bfloat16 [2, 24576, 6144], P('rep', 'col', 'row'), may hold values from -2 to 2
Outputs:
- mixed: bfloat16 [2, 512, 6144], P('rep', 'col', 'row')
- tally_in: bfloat16 [6144, 24576], P('row', 'col')
- tally_out: bfloat16 [24576, 6144], P('col', 'row')
All inputs are finite; a program needn't handle non-finite values.
Results may differ from a plain program's by a relative error of at most 0.0055.
Values may be sent and summed in bfloat16 or wider, within the bound.
A program may use at most 128 MiB of HBM per device.

v0:
```python
import math
import jax
import jax.numpy as jnp
from jax import lax
from jax.sharding import PartitionSpec as P

momentum_decay = 0.9
vote_scale = 0.3


def joined_along(blocks, dim):
    blocks = jnp.moveaxis(blocks, 0, dim)
    lengths = blocks.shape
    return blocks.reshape(*lengths[:dim], lengths[dim] * lengths[dim + 1], *lengths[dim + 2 :])


def sent_to_all(value, axis):
    copies = jnp.broadcast_to(value, (lax.axis_size(axis), *value.shape))
    return lax.all_to_all(copies, axis, split_axis=0, concat_axis=0, tiled=True)


def gather_directly(value, axis, dim):
    return joined_along(sent_to_all(value, axis), dim)


def cut_along(value, dim, peers):
    before, after = (value.shape[:dim], value.shape[dim + 1 :])
    return jnp.moveaxis(value.reshape(*before, peers, -1, *after), dim, 0)


def sum_at_owner(value, axis, dim):
    blocks = cut_along(value, dim, lax.axis_size(axis))
    arrived = lax.all_to_all(blocks, axis, split_axis=0, concat_axis=0, tiled=True)
    return arrived.sum(axis=0)


def gelu_value(pre):
    return 0.5 * pre * (1.0 + lax.erf(pre * (1.0 / math.sqrt(2.0))))


def gelu_slope(pre):
    return 0.5 * (1.0 + lax.erf(pre * (1.0 / math.sqrt(2.0)))) + pre * jnp.exp(-0.5 * pre * pre) * (
        1.0 / math.sqrt(2.0 * math.pi)
    )


def shards(patches, cotangent, w_in, w_out, moment_in, moment_out):
    inputs = gather_directly(patches[0], "col", 0)
    total_rows = inputs.shape[0]
    norm_factor = 1.0 / math.sqrt(total_rows)
    pre_whole = lax.psum(jnp.dot(inputs, w_in, preferred_element_type=jnp.float32), "row")
    hidden = gelu_value(pre_whole).astype(jnp.bfloat16)
    block = hidden
    mixed = sum_at_owner(
        jnp.dot(block, w_out, preferred_element_type=jnp.float32), "col", 0
    ).astype(jnp.bfloat16)
    grads = lax.all_gather(cotangent[0], "col", axis=0, tiled=True)
    block = grads
    back_whole = lax.psum(
        lax.dot_general(
            block, w_out, (((1,), (1,)), ((), ())), preferred_element_type=jnp.float32
        ).astype(jnp.bfloat16),
        "row",
    ).astype(jnp.float32)
    slope = (back_whole * gelu_slope(pre_whole)).astype(jnp.bfloat16)
    grad_first = (
        lax.dot_general(inputs, slope, (((0,), (0,)), ((), ())), preferred_element_type=jnp.float32)
        * norm_factor
    )
    grad_second = (
        lax.dot_general(hidden, grads, (((0,), (0,)), ((), ())), preferred_element_type=jnp.float32)
        * norm_factor
    )
    moved_first = (
        momentum_decay * moment_in[0].astype(jnp.float32) + (1.0 - momentum_decay) * grad_first
    )
    moved_second = (
        momentum_decay * moment_out[0].astype(jnp.float32) + (1.0 - momentum_decay) * grad_second
    )
    vote_first = jnp.tanh(moved_first / vote_scale).astype(jnp.bfloat16)
    vote_second = jnp.tanh(moved_second / vote_scale).astype(jnp.bfloat16)
    tally_first, tally_second = (
        lax.psum(vote_first, "rep").astype(jnp.float32),
        lax.psum(vote_second, "rep").astype(jnp.float32),
    )
    return (mixed[None], tally_first.astype(jnp.bfloat16), tally_second.astype(jnp.bfloat16))


def solution(mesh):
    in_specs = (
        P("rep", "col", "row"),
        P("rep", "col", "row"),
        P("row", "col"),
        P("col", "row"),
        P("rep", "row", "col"),
        P("rep", "col", "row"),
    )
    out_specs = (P("rep", "col", "row"), P("row", "col"), P("col", "row"))
    return jax.shard_map(shards, mesh=mesh, in_specs=in_specs, out_specs=out_specs, check_vma=False)
```

profile of v0, /device:TPU:1, one launch (start us, length us, event | category | flops | bytes accessed | tf_op | source)
XLA Modules:
  0.0 338.2 jit_solution(2649844550422343762)
XLA Ops:
  7.2 0.0 copy-start
  7.2 0.0 all-reduce.5.cloned.1.call-start
  7.2 1.0 broadcast_in_dim.4
  8.2 22.4 %all_to_all.10 = bf16[8,64,384]{2,1,0:T(8,128)(2,1)S(1)} all-to-all(bf16[8,64,384]{2,1,0:T(8,128)(2,1)S(1)} %broadcast_in_dim.4), channel_id=1, replica_groups=mesh['row'=16,'col'=8,'rep'=2] {'col'}, dimensions={0} | all-to-all | bytes 786432 | tf_op jit(solution)/shard_map/all_to_all | solution.py:19
  30.6 6.1 %fusion.20 = f32[512,3072]{1,0:T(8,128)} fusion(bf16[512,384]{1,0:T(8,128)(2,1)S(1)} %bitcast.36, bf16[384,3072]{1,0:T(8,128)(2,1)} %param.8), kind=kOutput, calls=%fused_computation.26 | convolution fusion | flops 1207959552 | bytes 9043968 | tf_op jit(solution)/shard_map/dot_general | solution.py:51
  36.7 0.0 copy-start.2
  36.7 0.0 all-reduce.5.cloned.1.call-update
  36.7 0.0 all-reduce.7.cloned.1.call-start
  36.8 0.7 copy-done.2
  37.5 20.5 %all-gather = bf16[1,512,384]{2,1,0:T(8,128)(2,1)S(1)} all-gather(bf16[1,64,384]{2,1,0:T(8,128)(2,1)S(1)} %copy-done.2), channel_id=2, replica_groups=mesh['row'=16,'col'=8,'rep'=2] {'col'}, dimensions={1}, use_global_device_ids=true | all-gather | bytes 442368 | tf_op jit(solution)/shard_map/all_gather | solution.py:57
  58.0 0.0 copy-done
  58.0 3.5 %convolution_convert_fusion = bf16[512,3072]{1,0:T(8,128)(2,1)} fusion(bf16[3072,384]{1,0:T(8,128)(2,1)S(1)} %copy-done, bf16[1,512,384]{2,1,0:T(8,128)(2,1)S(1)} %all-gather), kind=kOutput, calls=%fused_computation.17 | convolution fusion | flops 1209532416 | bytes 5898240 | tf_op jit(solution)/shard_map/dot_general | solution.py:60
  61.4 0.0 all-reduce.7.cloned.1.call-update
  61.5 0.0 all-reduce.9.cloned.1.call-start
  61.5 4.3 %copy.9 = bf16[1,384,3072]{1,2,0:T(8,128)(2,1)} copy(bf16[1,384,3072]{2,1,0:T(8,128)(2,1)} %param.10) | data formatting | bytes 4718592 | tf_op args[4]
  65.8 101.0 %all-reduce.5.cloned.1.call-done = f32[512,3072]{1,0:T(8,128)} async-done(((f32[512,3072]{1,0:T(8,128)}), f32[512,3072]{1,0:T(8,128)}) %all-reduce.5.cloned.1.call-update) | async-done | bytes 6291472 | tf_op jit(solution)/shard_map/psum | solution.py:51
  166.8 0.0 copy-start.3
  166.8 3.6 %multiply_convert_fusion = bf16[512,3072]{1,0:T(8,128)(2,1)S(1)} fusion(f32[512,3072]{1,0:T(8,128)} %all-reduce.5.cloned.1.call-done), kind=kLoop, calls=%fused_computation.7 | loop fusion | flops 7864320 | bytes 9437184 | tf_op jit(solution)/shard_map/convert_element_type | solution.py:52
  170.4 0.0 copy-start.1
  170.4 1.7 copy-done.1
  172.1 0.0 copy-done.3
  172.1 4.0 %fusion.8 = bf16[3072,384]{1,0:T(8,128)(2,1)} fusion(bf16[1,3072,384]{2,1,0:T(8,128)(2,1)S(1)} %copy-done.3, bf16[512,3072]{1,0:T(8,128)(2,1)S(1)} %multiply_convert_fusion, bf16[1,512,384]{2,1,0:T(8,128)(2,1)S(1)} %all-gather), kind=kOutput, calls=%fused_computation.12 | convolution fusion | flops 1215037440 | bytes 8257536 | tf_op jit(solution)/shard_map/dot_general | solution.py:71
  176.1 99.6 %all-reduce.7.cloned.1.call-done = bf16[512,3072]{1,0:T(8,128)(2,1)} async-done(((bf16[512,3072]{1,0:T(8,128)(2,1)}), bf16[512,3072]{1,0:T(8,128)(2,1)}) %all-reduce.7.cloned.1.call-update) | async-done | bytes 3145744 | tf_op jit(solution)/shard_map/psum | solution.py:59
  275.7 8.4 %fusion.11 = bf16[384,3072]{0,1:T(8,128)(2,1)} fusion(bf16[1,384,3072]{1,2,0:T(8,128)(2,1)} %copy.9, bf16[512,384]{1,0:T(8,128)(2,1)S(1)} %bitcast.37, f32[512,3072]{1,0:T(8,128)} %all-reduce.5.cloned.1.call-done, bf16[512,3072]{1,0:T(8,128)(2,1)} %all-reduce.7.cloned.1.call-done), kind=kOutput, calls=%fused_computation.16 | convolution fusion | flops 1232338944 | bytes 14548992 | tf_op jit(solution)/shard_map/dot_general | solution.py:67
  284.1 0.0 all-reduce.9.cloned.1.call-update
  284.1 3.7 %fusion.21 = f32[512,384]{1,0:T(8,128)S(1)} fusion(bf16[512,3072]{1,0:T(8,128)(2,1)} %copy-done.1, bf16[3072,384]{1,0:T(8,128)(2,1)S(1)} %copy-done), kind=kOutput, calls=%fused_computation.27 | convolution fusion | flops 1207959552 | bytes 6291456 | tf_op jit(solution)/shard_map/dot_general | solution.py:55
  287.8 27.9 %all_to_all.11 = f32[8,64,384]{2,1,0:T(8,128)S(1)} all-to-all(f32[8,64,384]{2,1,0:T(8,128)S(1)} %bitcast.38), channel_id=1, replica_groups=mesh['row'=16,'col'=8,'rep'=2] {'col'}, dimensions={0} | all-to-all | bytes 1572864 | tf_op jit(solution)/shard_map/all_to_all | solution.py:33
  315.7 0.7 reduce_sum.9
  316.4 7.7 %all-reduce.9.cloned.1.call-done = (bf16[384,3072]{0,1:T(8,128)(2,1)}, bf16[3072,384]{1,0:T(8,128)(2,1)}) async-done(((bf16[384,3072]{0,1:T(8,128)(2,1)}, bf16[3072,384]{1,0:T(8,128)(2,1)}), (bf16[384,3072]{0,1:T(8,128)(2,1)}, bf16[3072,384]{1,0:T(8,128)(2,1)})) %all-reduce.9.cloned.1.call-update) | async-done | bytes 4718608 | tf_op jit(solution)/shard_map/psum | solution.py:83
  324.1 4.3 %copy.10 = bf16[384,3072]{1,0:T(8,128)(2,1)} copy(bf16[384,3072]{0,1:T(8,128)(2,1)} %get-tuple-element.6) | data formatting | bytes 4718592
  328.4 3.3 copy.15
Async XLA Ops:
  7.2 50.8 %copy-start = (bf16[3072,384]{1,0:T(8,128)(2,1)S(1)}, bf16[3072,384]{1,0:T(8,128)(2,1)}, u32[]{:S(2)}) copy-start(bf16[3072,384]{1,0:T(8,128)(2,1)} %param.9) | copy-start | bytes 7077892
  7.2 159.7 %all-reduce.5.cloned.1.call-start = ((), (), s32[]{:S(2)}) async-start(), calls=%async_computation.2 | async-start | bytes 12582912 | tf_op jit(solution)/shard_map/psum | solution.py:51
  36.7 0.8 copy-start.2
  36.7 239.0 %all-reduce.7.cloned.1.call-start = ((), (), s32[]{:S(2)}) async-start(), calls=%async_computation.3 | async-start | bytes 6291456 | tf_op jit(solution)/shard_map/psum | solution.py:59
  61.5 262.7 %all-reduce.9.cloned.1.call-start = ((), (), s32[]{:S(2)}) async-start(), calls=%async_computation.4 | async-start | bytes 9437184 | tf_op jit(solution)/shard_map/psum | solution.py:83
  166.8 5.3 %copy-start.3 = (bf16[1,3072,384]{2,1,0:T(8,128)(2,1)S(1)}, bf16[1,3072,384]{2,1,0:T(8,128)(2,1)}, u32[]{:S(2)}) copy-start(bf16[1,3072,384]{2,1,0:T(8,128)(2,1)} %param.11) | copy-start | bytes 7077892
  170.4 1.7 copy-start.1
Sparse Core Ops, SparseCore 0:
  36.9 129.9 all-reduce.4
  170.2 105.4 all-reduce.6
  284.2 39.8 all-reduce.8
where the time goes:
time: 339 us; the launch traced here: 338 us
  waiting for transfers between devices  208 us (61%)
  blocking collectives  70.8 us (21%)
  matrix products  25.6 us (8%)
  local copies, waits for them, and re-layouts  15.3 us (5%)
  between operations  13.8 us (4%)
  other arithmetic  4.23 us (1%)
    psum x1, waiting for transfers between devices, shards(): lax.psum(jnp.dot(inputs, w_in, preferred_element_type=jnp.float32), 'row')  101 us
    psum x1, waiting for transfers between devices, shards(): lax.psum(lax.dot_general(block, w_out, (((1,), (1,)), ((), ())), preferre...  99.6 us
    all_to_all x1, blocking collectives, sum_at_owner(): lax.all_to_all(blocks, axis, split_axis=0, concat_axis=0, tiled=True)  27.9 us
    all_to_all x1, blocking collectives, sent_to_all(): return lax.all_to_all(copies, axis, split_axis=0, concat_axis=0, tiled=True)  22.4 us
    all_gather x1, blocking collectives, shards(): grads = lax.all_gather(cotangent[0], 'col', axis=0, tiled=True)  20.5 us
    unnamed x11, local copies, waits for them, and re-layouts  14.3 us
    dot_general x1, matrix products, shards(): lax.dot_general(inputs, slope, (((0,), (0,)), ((), ())), preferred_elemen...  8.39 us
    psum x1, waiting for transfers between devices, shards(): lax.psum(vote_first, 'rep').astype(jnp.float32)  7.74 us
  transfers between devices with their start and end apart: 3, of which 3 were waited for; matrix products, arithmetic and copies ran while one was open for 6% of the time, Pallas kernels for 0%

commit v1 on v0

--- a/solution.py
+++ b/solution.py
@@ -6,6 +6,11 @@
 
 momentum_decay = 0.9
 vote_scale = 0.3
+
+
+def tiled_gather(array, axis, dim):
+    copies = jnp.concatenate([array] * lax.axis_size(axis), axis=dim)
+    return lax.all_to_all(copies, axis, dim, dim, tiled=True)
 
 
 def joined_along(blocks, dim):
@@ -54,7 +59,7 @@
     mixed = sum_at_owner(
         jnp.dot(block, w_out, preferred_element_type=jnp.float32), "col", 0
     ).astype(jnp.bfloat16)
-    grads = lax.all_gather(cotangent[0], "col", axis=0, tiled=True)
+    grads = tiled_gather(cotangent[0], "col", 0)
     block = grads
     back_whole = lax.psum(
         lax.dot_general(

time: 339 us -> 339 us (level)
  waiting for transfers between devices: 208 us -> 215 us
  blocking collectives: 70.8 us -> 64.4 us
    all_gather x1 -> x0, blocking collectives: 20.5 us -> none  [shards(): grads = lax.all_gather(cotangent[0], 'col', axis=0, tiled=True)]
    all_to_all x0 -> x1, blocking collectives: none -> 14.1 us  [tiled_gather(): return lax.all_to_all(copies, axis, dim, dim, tiled=True)]
    psum x1, waiting for transfers between devices: 101 us -> 107 us  [shards(): lax.psum(jnp.dot(inputs, w_in, preferred_element_type=jnp.float32), 'row')]
    unnamed x11 -> x18, local copies, waits for them, and re-layouts: 14.3 us -> 14.4 us
where the time goes in v1:
time: 339 us; the launch traced here: 338 us
  waiting for transfers between devices  215 us (63%)
  blocking collectives  64.4 us (19%)
  matrix products  25.6 us (8%)
  local copies, waits for them, and re-layouts  15.4 us (5%)
  between operations  13.8 us (4%)
  other arithmetic  4.23 us (1%)
    psum x1, waiting for transfers between devices, shards(): lax.psum(jnp.dot(inputs, w_in, preferred_element_type=jnp.float32), 'row')  107 us
    psum x1, waiting for transfers between devices, shards(): lax.psum(lax.dot_general(block, w_out, (((1,), (1,)), ((), ())), preferre...  99.6 us
    all_to_all x1, blocking collectives, sum_at_owner(): lax.all_to_all(blocks, axis, split_axis=0, concat_axis=0, tiled=True)  27.9 us
    all_to_all x1, blocking collectives, sent_to_all(): return lax.all_to_all(copies, axis, split_axis=0, concat_axis=0, tiled=True)  22.4 us
    unnamed x18, local copies, waits for them, and re-layouts  14.4 us
    all_to_all x1, blocking collectives, tiled_gather(): return lax.all_to_all(copies, axis, dim, dim, tiled=True)  14.1 us
    dot_general x1, matrix products, shards(): lax.dot_general(inputs, slope, (((0,), (0,)), ((), ())), preferred_elemen...  8.39 us
    psum x1, waiting for transfers between devices, shards(): lax.psum(vote_first, 'rep').astype(jnp.float32)  7.74 us
  transfers between devices with their start and end apart: 3, of which 3 were waited for; matrix products, arithmetic and copies ran while one was open for 6% of the time, Pallas kernels for 0%

profile of v1, /device:TPU:1, one launch (start us, length us, event | category | flops | bytes accessed | tf_op | source)
XLA Modules:
  0.0 338.2 jit_solution(2819725202058421522)
XLA Ops:
  7.2 0.0 copy-start
  7.2 0.0 all-reduce.5.cloned.1.call-start
  7.2 1.0 broadcast_in_dim.4
  8.2 22.4 %all_to_all.22 = bf16[8,64,384]{2,1,0:T(8,128)(2,1)S(1)} all-to-all(bf16[8,64,384]{2,1,0:T(8,128)(2,1)S(1)} %broadcast_in_dim.4), channel_id=1, replica_groups=mesh['row'=16,'col'=8,'rep'=2] {'col'}, dimensions={0} | all-to-all | bytes 786432 | tf_op jit(solution)/shard_map/all_to_all | solution.py:24
  30.6 6.1 %fusion.18 = f32[512,3072]{1,0:T(8,128)} fusion(bf16[512,384]{1,0:T(8,128)(2,1)S(1)} %bitcast.44, bf16[384,3072]{1,0:T(8,128)(2,1)} %param.8), kind=kOutput, calls=%fused_computation.32 | convolution fusion | flops 1207959552 | bytes 9043968 | tf_op jit(solution)/shard_map/dot_general | solution.py:56
  36.7 0.0 copy-start.1
  36.7 0.0 all-reduce.5.cloned.1.call-update
  36.7 0.0 all-reduce.7.cloned.1.call-start
  36.8 0.7 copy-done.1
  37.6 14.1 %all_to_all.23 = bf16[8,64,384]{2,1,0:T(8,128)(2,1)S(1)} all-to-all(bf16[8,64,384]{2,1,0:T(8,128)(2,1)S(1)} %bitcast.47), channel_id=1, replica_groups=mesh['row'=16,'col'=8,'rep'=2] {'col'}, dimensions={0} | all-to-all | bytes 786432 | tf_op jit(solution)/shard_map/all_to_all | solution.py:13
  51.8 0.0 copy-done
  51.8 3.5 %convolution_convert_fusion = bf16[512,3072]{1,0:T(8,128)(2,1)} fusion(bf16[512,384]{1,0:T(8,128)(2,1)S(1)} %bitcast.48, bf16[3072,384]{1,0:T(8,128)(2,1)S(1)} %copy-done), kind=kOutput, calls=%fused_computation.17 | convolution fusion | flops 1209532416 | bytes 5898240 | tf_op jit(solution)/shard_map/dot_general | solution.py:65
  55.2 0.0 all-reduce.7.cloned.1.call-update
  55.3 0.0 all-reduce.9.cloned.1.call-start
  55.3 4.3 %copy.9 = bf16[1,384,3072]{1,2,0:T(8,128)(2,1)} copy(bf16[1,384,3072]{2,1,0:T(8,128)(2,1)} %param.10) | data formatting | bytes 4718592 | tf_op args[4]
  59.6 107.2 %all-reduce.5.cloned.1.call-done = f32[512,3072]{1,0:T(8,128)} async-done(((f32[512,3072]{1,0:T(8,128)}), f32[512,3072]{1,0:T(8,128)}) %all-reduce.5.cloned.1.call-update) | async-done | bytes 6291472 | tf_op jit(solution)/shard_map/psum | solution.py:56
  166.8 0.0 copy-start.3
  166.8 3.6 %multiply_convert_fusion = bf16[512,3072]{1,0:T(8,128)(2,1)S(1)} fusion(f32[512,3072]{1,0:T(8,128)} %all-reduce.5.cloned.1.call-done), kind=kLoop, calls=%fused_computation.7 | loop fusion | flops 7864320 | bytes 9437184 | tf_op jit(solution)/shard_map/convert_element_type | solution.py:57
  170.4 0.0 copy-start.2
  170.4 1.7 copy-done.2
  172.1 0.0 copy-done.3
  172.1 4.0 %fusion.8 = bf16[3072,384]{1,0:T(8,128)(2,1)} fusion(bf16[1,3072,384]{2,1,0:T(8,128)(2,1)S(1)} %copy-done.3, bf16[512,3072]{1,0:T(8,128)(2,1)S(1)} %multiply_convert_fusion, bf16[512,384]{1,0:T(8,128)(2,1)S(1)} %bitcast.49), kind=kOutput, calls=%fused_computation.12 | convolution fusion | flops 1215037440 | bytes 8257536 | tf_op jit(solution)/shard_map/dot_general | solution.py:76
  176.1 99.6 %all-reduce.7.cloned.1.call-done = bf16[512,3072]{1,0:T(8,128)(2,1)} async-done(((bf16[512,3072]{1,0:T(8,128)(2,1)}), bf16[512,3072]{1,0:T(8,128)(2,1)}) %all-reduce.7.cloned.1.call-update) | async-done | bytes 3145744 | tf_op jit(solution)/shard_map/psum | solution.py:64
  275.7 8.4 %fusion.11 = bf16[384,3072]{0,1:T(8,128)(2,1)} fusion(bf16[1,384,3072]{1,2,0:T(8,128)(2,1)} %copy.9, bf16[512,384]{1,0:T(8,128)(2,1)S(1)} %bitcast.45, f32[512,3072]{1,0:T(8,128)} %all-reduce.5.cloned.1.call-done, bf16[512,3072]{1,0:T(8,128)(2,1)} %all-reduce.7.cloned.1.call-done), kind=kOutput, calls=%fused_computation.16 | convolution fusion | flops 1232338944 | bytes 14548992 | tf_op jit(solution)/shard_map/dot_general | solution.py:72
  284.1 0.0 all-reduce.9.cloned.1.call-update
  284.1 3.7 %fusion.19 = f32[512,384]{1,0:T(8,128)S(1)} fusion(bf16[512,3072]{1,0:T(8,128)(2,1)} %copy-done.2, bf16[3072,384]{1,0:T(8,128)(2,1)S(1)} %copy-done), kind=kOutput, calls=%fused_computation.33 | convolution fusion | flops 1207959552 | bytes 6291456 | tf_op jit(solution)/shard_map/dot_general | solution.py:60
  287.8 27.9 %all_to_all.24 = f32[8,64,384]{2,1,0:T(8,128)S(1)} all-to-all(f32[8,64,384]{2,1,0:T(8,128)S(1)} %bitcast.46), channel_id=1, replica_groups=mesh['row'=16,'col'=8,'rep'=2] {'col'}, dimensions={0} | all-to-all | bytes 1572864 | tf_op jit(solution)/shard_map/all_to_all | solution.py:38
  315.7 0.7 reduce_sum.9
  316.4 7.7 %all-reduce.9.cloned.1.call-done = (bf16[384,3072]{0,1:T(8,128)(2,1)}, bf16[3072,384]{1,0:T(8,128)(2,1)}) async-done(((bf16[384,3072]{0,1:T(8,128)(2,1)}, bf16[3072,384]{1,0:T(8,128)(2,1)}), (bf16[384,3072]{0,1:T(8,128)(2,1)}, bf16[3072,384]{1,0:T(8,128)(2,1)})) %all-reduce.9.cloned.1.call-update) | async-done | bytes 4718608 | tf_op jit(solution)/shard_map/psum | solution.py:88
  324.1 4.3 %copy.10 = bf16[384,3072]{1,0:T(8,128)(2,1)} copy(bf16[384,3072]{0,1:T(8,128)(2,1)} %get-tuple-element.6) | data formatting | bytes 4718592
  328.4 3.3 copy.22
  (8 shorter events, 0.1 us)
Async XLA Ops:
  7.2 44.6 %copy-start = (bf16[3072,384]{1,0:T(8,128)(2,1)S(1)}, bf16[3072,384]{1,0:T(8,128)(2,1)}, u32[]{:S(2)}) copy-start(bf16[3072,384]{1,0:T(8,128)(2,1)} %param.9) | copy-start | bytes 7077892
  7.2 159.7 %all-reduce.5.cloned.1.call-start = ((), (), s32[]{:S(2)}) async-start(), calls=%async_computation.3 | async-start | bytes 12582912 | tf_op jit(solution)/shard_map/psum | solution.py:56
  36.7 0.8 copy-start.1
  36.7 239.0 %all-reduce.7.cloned.1.call-start = ((), (), s32[]{:S(2)}) async-start(), calls=%async_computation.4 | async-start | bytes 6291456 | tf_op jit(solution)/shard_map/psum | solution.py:64
  55.3 268.9 %all-reduce.9.cloned.1.call-start = ((), (), s32[]{:S(2)}) async-start(), calls=%async_computation.5 | async-start | bytes 9437184 | tf_op jit(solution)/shard_map/psum | solution.py:88
  166.8 5.3 %copy-start.3 = (bf16[1,3072,384]{2,1,0:T(8,128)(2,1)S(1)}, bf16[1,3072,384]{2,1,0:T(8,128)(2,1)}, u32[]{:S(2)}) copy-start(bf16[1,3072,384]{2,1,0:T(8,128)(2,1)} %param.11) | copy-start | bytes 7077892
  170.4 1.7 copy-start.2
Sparse Core Ops, SparseCore 0:
  36.9 129.9 all-reduce.4
  170.2 105.4 all-reduce.6
  284.2 39.8 all-reduce.8
